TPU v7x, 32 devices: a whole 2x2x4 slice. The times are simulated.
32 devices in a mesh: ep: 8 (over z, y), tp: 4 (over x, core).
Axes of the slice: x: 2, y: 2, z: 4, core: 2. Of those that a mesh axis runs over, the one named last changes fastest.
Arguments:
- tokens: bfloat16 [4096, 2048], P(('ep', 'tp')), may hold values from -6 to 6
- norm_gain: float32 [2048], replicated, may hold values from 0.1 to 1.9
- expert_ids: int32 [4096, 6], P(('ep', 'tp')), may hold values from 0 to 15, as said below
- slot_index: int32 [4096, 6], P(('ep', 'tp')), may hold values from 0 to 63, as said below
- dropped: int32 [4096, 6], P(('ep', 'tp')), may hold values from 0 to 1, as said below
- gates: float32 [4096, 6], P(('ep', 'tp')), may hold values from 0.05 to 0.8
- w_gate: bfloat16 [16, 2048, 704], P('ep', None, 'tp'), may hold values from -0.125 to 0.125
- w_up: bfloat16 [16, 2048, 704], P('ep', None, 'tp'), may hold values from -0.125 to 0.125
- w_down: bfloat16 [16, 2048, 704], P('ep', None, 'tp'), may hold values from -0.21875 to 0.21875
- shared_gate: bfloat16 [2048, 1408], P(None, 'tp'), may hold values from -0.125 to 0.125
- shared_up: bfloat16 [2048, 1408], P(None, 'tp'), may hold values from -0.125 to 0.125
- shared_down: bfloat16 [1408, 2048], replicated, may hold values from -0.15625 to 0.15625
Outputs:
- layer_out: bfloat16 [4096, 2048], P(('ep', 'tp'))
Inputs may be any that keep to these rules, and one draw needn't show every extreme that they name: `expert_ids`: each token names 6 different experts; some expert has 64 kept pairs from the tokens of every device. `slot_index`: for a kept pair, its place among the slots of its expert for the tokens of its device (the tokens n with one value of n // 128); the kept pairs of one device and one expert have distinct places; 0 for a dropped pair. `dropped`: 1 for the pairs of a device and an expert beyond the 64 that are kept.
All inputs are finite; a program needn't handle non-finite values.
Results may differ from a plain program's by a relative error of at most 0.0054.
Values may be sent and summed in bfloat16 or wider, within the bound.
A program may use at most 128 MiB of HBM per device.

v0:
```python
import jax
import jax.numpy as jnp
from jax import lax
from jax.sharding import PartitionSpec as P

TOP = 6
EXP_DEV = 2
TOK_DEV = 128
norm_eps = 1e-06


def swiglu(left, right):
    return jax.nn.silu(left) * right


def on_device(
    tokens,
    norm_gain,
    expert_ids,
    slot_index,
    dropped,
    gates,
    w_gate,
    w_up,
    w_down,
    shared_gate,
    shared_up,
    shared_down,
):
    n_expert_groups = lax.axis_size("ep")
    experts = EXP_DEV * n_expert_groups
    capacity = TOK_DEV * TOP * 4 // (experts * 3)
    model_width = tokens.shape[1]
    local_rows = tokens.shape[0]
    values = tokens.astype(jnp.float32)
    scale = lax.rsqrt(jnp.mean(values * values, axis=-1, keepdims=True) + norm_eps)
    normed = (values * scale * norm_gain).astype(jnp.bfloat16)
    destination_position = expert_ids * capacity + slot_index
    kept_pair = dropped == 0
    matrix_breadth = lax.iota(jnp.int32, experts * capacity)
    matches = (destination_position[:, :, None] == matrix_breadth[None, None, :]) & kept_pair[
        :, :, None
    ]
    dispatch_table = jnp.any(matches, axis=1).astype(jnp.bfloat16)
    outgoing = lax.dot_general(
        dispatch_table, normed, (((0,), (0,)), ((), ())), preferred_element_type=jnp.float32
    ).astype(jnp.bfloat16)
    boxes = outgoing.reshape(n_expert_groups, EXP_DEV, capacity, model_width)
    received = lax.all_to_all(boxes, "ep", split_axis=0, concat_axis=0, tiled=True)
    gate_all = lax.all_gather(w_gate, "tp", axis=2, tiled=True)
    up_all = lax.all_gather(w_up, "tp", axis=2, tiled=True)
    down_all = lax.all_gather(w_down, "tp", axis=2, tiled=True)
    gate_act = jnp.einsum("iecd,edf->iecf", received, gate_all, preferred_element_type=jnp.float32)
    up_act = jnp.einsum("iecd,edf->iecf", received, up_all, preferred_element_type=jnp.float32)
    hidden = swiglu(gate_act, up_act).astype(jnp.bfloat16)
    expert_out = jnp.einsum(
        "iecf,edf->iecd", hidden, down_all, preferred_element_type=jnp.float32
    ).astype(jnp.bfloat16)
    returned_output = lax.all_to_all(expert_out, "ep", split_axis=0, concat_axis=0, tiled=True)
    returned_rows = returned_output.reshape(experts * capacity, model_width)
    shard_piece = lax.all_gather(normed, "tp", axis=0, tiled=True)
    gate_act = jnp.dot(shard_piece, shared_gate, preferred_element_type=jnp.float32)
    up_act = jnp.dot(shard_piece, shared_up, preferred_element_type=jnp.float32)
    partial_hidden = swiglu(gate_act, up_act).astype(jnp.bfloat16)
    whole_hidden = lax.all_to_all(partial_hidden, "tp", split_axis=0, concat_axis=1, tiled=True)
    shared_out = jnp.dot(whole_hidden, shared_down, preferred_element_type=jnp.float32)
    safe_target = jnp.where(kept_pair, destination_position, 0)
    picked = jnp.take(returned_rows, safe_target.reshape(-1), axis=0).reshape(
        local_rows, TOP, model_width
    )
    kept_weights = jnp.where(kept_pair, gates, jnp.float32(0.0))
    routed = jnp.sum(picked.astype(jnp.float32) * kept_weights[:, :, None], axis=1)
    return (values + shared_out + routed).astype(jnp.bfloat16)


def solution(mesh):
    placed = (
        P(("ep", "tp"), None),
        P(),
        P(("ep", "tp"), None),
        P(("ep", "tp"), None),
        P(("ep", "tp"), None),
        P(("ep", "tp"), None),
        P("ep", None, "tp"),
        P("ep", None, "tp"),
        P("ep", None, "tp"),
        P(None, "tp"),
        P(None, "tp"),
        P(),
    )
    return jax.shard_map(
        on_device, mesh=mesh, in_specs=placed, out_specs=P(("ep", "tp"), None), check_vma=False
    )
```

profile of v0, /device:TPU:0, one launch (start us, length us, event | category | flops | bytes accessed | tf_op | source)
XLA Modules:
  0.0 298.9 jit_solution(15551164740821854965)
XLA Ops:
  6.5 0.0 copy-start
  6.5 0.0 copy-start.1
  6.5 0.0 copy-start.3
  6.5 0.0 copy-start.6
  6.5 0.0 copy-start.7
  6.6 0.0 all-gather.9.cloned.1.call-start
  6.6 0.7 all-gather.9.cloned.1.call-update
  7.3 0.0 all-gather.11.cloned.1.call-start
  7.3 0.7 all-gather.11.cloned.1.call-update
  8.0 0.0 all-gather.7.cloned.1.call-start
  8.1 0.7 all-gather.7.cloned.1.call-update
  8.8 0.0 copy-done.1
  8.8 0.2 fusion.29
  9.0 0.0 copy-done.3
  9.0 0.2 fusion.31
  9.2 0.0 copy-start.2
  9.2 0.0 copy-done.6
  9.2 0.0 copy-done.5
  9.2 0.0 copy-done.7
  9.3 0.6 fusion.15
  9.9 1.3 convolution_convert_fusion
  11.2 100.4 %all_to_all.29 = bf16[8,2,64,2048]{3,2,1,0:T(8,128)(2,1)} all-to-all(bf16[8,2,64,2048]{3,2,1,0:T(8,128)(2,1)S(1)} %bitcast.62), channel_id=1, replica_groups=mesh['ep'=8,'tp'=4] {'ep'}, dimensions={0} | all-to-all | bytes 8388608 | tf_op jit(solution)/shard_map/all_to_all | solution.py:49
  111.5 0.0 copy-done.2
  111.5 9.2 %fusion.2 = f32[2,8,64,704]{3,2,1,0:T(8,128)} fusion(bf16[2,2048,704]{1,2,0:T(8,128)(2,1)} %all-gather.9.cloned.1.call-done, bf16[8,2,64,2048]{3,2,1,0:T(8,128)(2,1)} %all_to_all.29), kind=kOutput, calls=%fused_computation.4 | convolution fusion | flops 2952790016 | bytes 12845056 | tf_op jit(solution)/shard_map/iecd,edf->iecf/dot_general | solution.py:54
  120.7 24.3 %all-gather.7.cloned.1.call-done = bf16[2,2048,704]{1,2,0:T(8,128)(2,1)} async-done(((bf16[2,2048,176]{1,2,0:T(8,128)(2,1)}), bf16[2,2048,704]{1,2,0:T(8,128)(2,1)}) %all-gather.7.cloned.1.call-update) | async-done | bytes 5767184 | tf_op jit(solution)/shard_map/all_gather | solution.py:50
  145.0 13.1 %convert_bitcast_fusion = bf16[8,2,64,2048]{3,2,0,1:T(8,128)(2,1)} fusion(bf16[2,2048,704]{1,2,0:T(8,128)(2,1)} %all-gather.11.cloned.1.call-done, f32[2,8,64,704]{3,2,1,0:T(8,128)} %fusion.2, bf16[2,2048,704]{1,2,0:T(8,128)(2,1)} %all-gather.7.cloned.1.call-done, bf16[8,2,64,2048]{3,2,1,0:T(8,128)(2,1)} %all_to_all.29), kind=kOutput, calls=%fused_computation.8 | convolution fusion | flops 5912002560 | bytes 22806528 | tf_op jit(solution)/shard_map/iecf,edf->iecd/dot_general | solution.py:56
  158.1 4.7 %copy.39 = bf16[8,2,64,2048]{3,2,1,0:T(8,128)(2,1)} copy(bf16[8,2,64,2048]{3,2,0,1:T(8,128)(2,1)} %convert_bitcast_fusion) | data formatting | bytes 8388608 | tf_op jit(solution)/shard_map/convert_element_type | solution.py:58
  162.9 5.6 %all-to-all-start.2 = ((bf16[8,2,64,2048]{3,2,1,0:T(8,128)(2,1)}), bf16[8,2,64,2048]{3,2,1,0:T(8,128)(2,1)}, u32[]{:S(2)}, u32[]{:S(2)}) async-start(bf16[8,2,64,2048]{3,2,1,0:T(8,128)(2,1)} %copy.39), calls=%async_computation.2 | async-start | bytes 8388608 | tf_op jit(solution)/shard_map/all_to_all | solution.py:59
  168.5 0.0 all-gather.5.cloned.1.call-start
  168.6 0.5 all-gather.5.cloned.1.call-update
  169.1 0.1 copy.40
  169.2 0.1 reshape.66
  169.4 0.0 copy-done.4
  169.4 0.1 copy.41
  169.5 0.1 copy.36
  169.7 24.0 %all-gather.5.cloned.1.call-done = bf16[512,2048]{1,0:T(8,128)(2,1)} async-done(((bf16[128,2048]{1,0:T(8,128)(2,1)}), bf16[512,2048]{1,0:T(8,128)(2,1)}) %all-gather.5.cloned.1.call-update) | async-done | bytes 2097168 | tf_op jit(solution)/shard_map/all_gather | solution.py:61
  193.7 0.0 copy-done
  193.7 2.7 fusion.34
  196.4 0.0 copy-done.8
  196.4 2.4 fusion.28
  198.8 0.8 copy.55
  199.6 62.6 %all-to-all-done.2 = bf16[8,2,64,2048]{3,2,1,0:T(8,128)(2,1)} async-done(((bf16[8,2,64,2048]{3,2,1,0:T(8,128)(2,1)}), bf16[8,2,64,2048]{3,2,1,0:T(8,128)(2,1)}, u32[]{:S(2)}, u32[]{:S(2)}) %all-to-all-start.2) | async-done | bytes 4194336 | tf_op jit(solution)/shard_map/all_to_all | solution.py:59
  262.2 3.6 %all-to-all-start = ((bf16[4,128,352]{1,2,0:T(8,128)(2,1)}), bf16[4,128,352]{1,2,0:T(8,128)(2,1)S(1)}, u32[]{:S(2)}, u32[]{:S(2)}) async-start(bf16[4,128,352]{1,2,0:T(8,128)(2,1)} %bitcast.61), calls=%async_computation | async-start | bytes 720896 | tf_op jit(solution)/shard_map/all_to_all | solution.py:65
  265.9 9.9 %gather_fusion = bf16[768,2048]{1,0:T(8,128)(2,1)} fusion(bf16[1024,2048]{1,0:T(8,128)(2,1)} %bitcast.12, s32[1024]{0:T(1024)S(1)} %pad_clamp_fusion), kind=kCustom, calls=%fused_computation | custom fusion | bytes 6294528 | tf_op jit(solution)/shard_map/jit(_take)/gather | solution.py:68
  275.7 6.2 %gather.7 = bf16[128,6,2048]{2,1,0:T(8,128)(2,1)} reshape(bf16[768,2048]{1,0:T(8,128)(2,1)} %gather_fusion) | data formatting | bytes 6291456 | tf_op jit(solution)/shard_map/jit(_take)/gather | solution.py:68
  282.0 6.0 %multiply_reduce_fusion = f32[128,2048]{1,0:T(8,128)S(1)} fusion(f32[128,6]{1,0:T(8,128)S(1)} %copy.41, bf16[128,6,2048]{2,1,0:T(8,128)(2,1)} %gather.7, pred[128,6]{1,0:T(8,128)(4,1)S(1)} %copy.36), kind=kLoop, calls=%fused_computation.1 | loop fusion | flops 6029312 | bytes 4198144 | tf_op jit(solution)/shard_map/reduce_sum | solution.py:72
  287.9 0.0 all-to-all-done
  287.9 4.4 %fusion.17 = bf16[128,2048]{1,0:T(8,128)(2,1)} fusion(f32[128,2048]{1,0:T(8,128)S(1)} %multiply_reduce_fusion, bf16[128,1408]{0,1:T(8,128)(2,1)S(1)} %bitcast.63, bf16[1408,2048]{1,0:T(8,128)(2,1)} %param.23, bf16[128,2048]{1,0:T(8,128)(2,1)S(1)} %copy-done.1), kind=kOutput, calls=%fused_computation.24 | convolution fusion | flops 739246080 | bytes 8224768 | tf_op jit(solution)/shard_map/dot_general | solution.py:66
  (10 shorter events, 0.1 us)
Async XLA Ops:
  6.5 187.1 %copy-start = (bf16[2048,352]{0,1:T(8,128)(2,1)S(1)}, bf16[2048,352]{0,1:T(8,128)(2,1)}, u32[]{:S(2)}) copy-start(bf16[2048,352]{0,1:T(8,128)(2,1)} %param.21) | copy-start | bytes 4325380
  6.5 2.2 copy-start.1
  6.5 2.4 copy-start.3
  6.5 2.7 copy-start.6
  6.5 2.7 copy-start.5
  6.5 2.7 copy-start.7
  6.6 105.0 %all-gather.9.cloned.1.call-start = ((), (), s32[]{:S(2)}) async-start(), calls=%async_computation.5 | async-start | bytes 7208960 | tf_op jit(solution)/shard_map/all_gather | solution.py:51
  7.3 113.4 %all-gather.11.cloned.1.call-start = ((), (), s32[]{:S(2)}) async-start(), calls=%async_computation.6 | async-start | bytes 7208960 | tf_op jit(solution)/shard_map/all_gather | solution.py:52
  8.0 137.0 %all-gather.7.cloned.1.call-start = ((), (), s32[]{:S(2)}) async-start(), calls=%async_computation.4 | async-start | bytes 7208960 | tf_op jit(solution)/shard_map/all_gather | solution.py:50
  9.2 102.4 %copy-start.2 = (bf16[128,2048]{1,0:T(8,128)(2,1)}, bf16[128,2048]{1,0:T(8,128)(2,1)S(1)}, u32[]{:S(2)}) copy-start(bf16[128,2048]{1,0:T(8,128)(2,1)S(1)} %fusion.31) | copy-start | bytes 1572868
  162.9 6.5 %copy-start.4 = (f32[128,6]{0,1:T(8,128)S(1)}, f32[128,6]{0,1:T(8,128)}, u32[]{:S(2)}) copy-start(f32[128,6]{0,1:T(8,128)} %param.17) | copy-start | bytes 9220
  162.9 99.3 %all-to-all-start.2 = ((bf16[8,2,64,2048]{3,2,1,0:T(8,128)(2,1)}), bf16[8,2,64,2048]{3,2,1,0:T(8,128)(2,1)}, u32[]{:S(2)}, u32[]{:S(2)}) async-start(bf16[8,2,64,2048]{3,2,1,0:T(8,128)(2,1)} %copy.39), calls=%async_computation.2 | async-start | bytes 8388608 | tf_op jit(solution)/shard_map/all_to_all | solution.py:59
  168.5 25.1 %all-gather.5.cloned.1.call-start = ((), (), s32[]{:S(2)}) async-start(), calls=%async_computation.3 | async-start | bytes 2621440 | tf_op jit(solution)/shard_map/all_gather | solution.py:61
  193.7 2.7 copy-start.8
  262.2 25.7 %all-to-all-start = ((bf16[4,128,352]{1,2,0:T(8,128)(2,1)}), bf16[4,128,352]{1,2,0:T(8,128)(2,1)S(1)}, u32[]{:S(2)}, u32[]{:S(2)}) async-start(bf16[4,128,352]{1,2,0:T(8,128)(2,1)} %bitcast.61), calls=%async_computation | async-start | bytes 720896 | tf_op jit(solution)/shard_map/all_to_all | solution.py:65
Sparse Core Ops, SparseCore 0:
  8.9 46.0 all-gather.8
  56.6 43.3 all-gather.10
  101.6 43.3 all-gather.6
  170.6 23.0 all-gather.4
where the time goes:
time: 300 us; the launch traced here: 299 us
  waiting for transfers between devices  114 us (38%)
  blocking collectives  100 us (33%)
  matrix products  33.2 us (11%)
  local copies, waits for them, and re-layouts  22.2 us (7%)
  between operations  13.3 us (4%)
  starting transfers between devices  9.44 us (3%)
  other arithmetic  6.97 us (2%)
    all_to_all x1, blocking collectives, on_device(): lax.all_to_all(boxes, 'ep', split_axis=0, concat_axis=0, tiled=True)  100 us
    all_to_all x1, waiting for transfers between devices, on_device(): lax.all_to_all(expert_out, 'ep', split_axis=0, concat_axis=0, tiled=True)  62.6 us
    all_gather x1, waiting for transfers between devices, on_device(): gate_all = lax.all_gather(w_gate, 'tp', axis=2, tiled=True)  24.3 us
    all_gather x1, waiting for transfers between devices, on_device(): shard_piece = lax.all_gather(normed, 'tp', axis=0, tiled=True)  24 us
    gather x2, local copies, waits for them, and re-layouts, on_device(): jnp.take(returned_rows, safe_target.reshape(-1), axis=0)  16.1 us
    dot_general x1, matrix products, on_device(): jnp.einsum('iecf,edf->iecd', hidden, down_all, preferred_element_type=jnp...  13.1 us
    dot_general x1, matrix products, on_device(): jnp.einsum('iecd,edf->iecf', received, up_all, preferred_element_type=jnp...  9.17 us
  transfers between devices with their start and end apart: 6, of which 3 were waited for; matrix products, arithmetic and copies ran while one was open for 13% of the time, Pallas kernels for 0%

commit v1 on v0

--- a/solution.py
+++ b/solution.py
@@ -58,7 +58,14 @@
     ).astype(jnp.bfloat16)
     returned_output = lax.all_to_all(expert_out, "ep", split_axis=0, concat_axis=0, tiled=True)
     returned_rows = returned_output.reshape(experts * capacity, model_width)
-    shard_piece = lax.all_gather(normed, "tp", axis=0, tiled=True)
+    n_dev = lax.axis_size("tp")
+    hops = [(i, (i + 1) % n_dev) for i in range(n_dev)]
+    pieces = [normed]
+    for far in range(1, n_dev):
+        pieces = [lax.ppermute(pieces[0], "tp", hops), *pieces]
+    full = jnp.concatenate(pieces, axis=0)
+    shift = (lax.axis_index("tp") + 1) * pieces[-1].shape[0]
+    shard_piece = jnp.roll(full, shift, axis=0)
     gate_act = jnp.dot(shard_piece, shared_gate, preferred_element_type=jnp.float32)
     up_act = jnp.dot(shard_piece, shared_up, preferred_element_type=jnp.float32)
     partial_hidden = swiglu(gate_act, up_act).astype(jnp.bfloat16)

time: 300 us -> 299 us (level)
  local copies, waits for them, and re-layouts: 22.2 us -> 26.3 us
  waiting for transfers between devices: 114 us -> 110 us
  matrix products: 33.2 us -> 29.9 us
  other arithmetic: 6.97 us -> 10.1 us
    all_gather x1, waiting for transfers between devices: 24.3 us -> 0.01 us  [on_device(): gate_all = lax.all_gather(w_gate, 'tp', axis=2, tiled=True)]
    all_gather x1 -> x0, waiting for transfers between devices: 24 us -> none  [on_device(): shard_piece = lax.all_gather(normed, 'tp', axis=0, tiled=True)]
    all_gather x1, waiting for transfers between devices: 0.01 us -> 23.4 us  [on_device(): down_all = lax.all_gather(w_down, 'tp', axis=2, tiled=True)]
    ppermute x0 -> x3, waiting for transfers between devices: none -> 21.2 us  [on_device(): pieces = [lax.ppermute(pieces[0], 'tp', hops), *pieces]]
  transfers between devices with their start and end apart: 6 -> 8, of which waited for: 3 -> 5; matrix products, arithmetic and copies ran while one was open for 13% -> 15% of each run, Pallas kernels for 0% -> 0%
where the time goes in v1:
time: 299 us
  waiting for transfers between devices  110 us (37%)
  blocking collectives  100 us (33%)
  matrix products  29.9 us (10%)
  local copies, waits for them, and re-layouts  26.3 us (9%)
  between operations  13.3 us (4%)
  other arithmetic  10.1 us (3%)
  starting transfers between devices  9.1 us (3%)
    all_to_all x1, blocking collectives, on_device(): lax.all_to_all(boxes, 'ep', split_axis=0, concat_axis=0, tiled=True)  100 us
    all_to_all x1, waiting for transfers between devices, on_device(): lax.all_to_all(expert_out, 'ep', split_axis=0, concat_axis=0, tiled=True)  62.9 us
    all_gather x1, waiting for transfers between devices, on_device(): down_all = lax.all_gather(w_down, 'tp', axis=2, tiled=True)  23.4 us
    ppermute x3, waiting for transfers between devices, on_device(): pieces = [lax.ppermute(pieces[0], 'tp', hops), *pieces]  21.2 us
    gather x2, local copies, waits for them, and re-layouts, on_device(): jnp.take(returned_rows, safe_target.reshape(-1), axis=0)  16.1 us
    dot_general x1, matrix products, on_device(): jnp.einsum('iecf,edf->iecd', hidden, down_all, preferred_element_type=jnp...  13.1 us
    dot_general x1, matrix products, on_device(): jnp.einsum('iecd,edf->iecf', received, up_all, preferred_element_type=jnp...  8.98 us
  transfers between devices with their start and end apart: 8, of which 5 were waited for; matrix products, arithmetic and copies ran while one was open for 15% of the time, Pallas kernels for 0%

profile of v1, /device:TPU:0, one launch (start us, length us, event | category | flops | bytes accessed | tf_op | source)
XLA Modules:
  0.0 298.7 jit_solution(5645106279037805128)
XLA Ops:
  6.5 0.0 copy-start
  6.5 0.0 copy-start.9
  6.6 0.0 all-gather.6.cloned.1.call-start
  6.6 0.7 all-gather.6.cloned.1.call-update
  7.3 0.0 all-gather.4.cloned.1.call-start
  7.3 0.7 all-gather.4.cloned.1.call-update
  8.0 0.0 all-gather.8.cloned.1.call-start
  8.1 0.7 all-gather.8.cloned.1.call-update
  8.8 0.0 copy-done.1
  8.8 0.2 fusion.31
  9.0 0.6 copy-done.6
  9.6 0.0 copy-done.3
  9.6 0.2 fusion.33
  9.8 0.6 compare_and_fusion
  10.4 0.6 fusion.15
  11.0 1.3 convolution_convert_fusion
  12.3 100.4 %all_to_all.29 = bf16[8,2,64,2048]{3,2,1,0:T(8,128)(2,1)} all-to-all(bf16[8,2,64,2048]{3,2,1,0:T(8,128)(2,1)S(1)} %bitcast.60), channel_id=1, replica_groups=mesh['ep'=8,'tp'=4] {'ep'}, dimensions={0} | all-to-all | bytes 8388608 | tf_op jit(solution)/shard_map/all_to_all | solution.py:49
  112.7 0.0 copy-done.5
  112.7 9.0 %fusion.2 = f32[2,8,64,704]{3,2,1,0:T(8,128)} fusion(bf16[2,2048,704]{1,2,0:T(8,128)(2,1)} %all-gather.6.cloned.1.call-done, bf16[8,2,64,2048]{3,2,1,0:T(8,128)(2,1)} %all_to_all.29), kind=kOutput, calls=%fused_computation.4 | convolution fusion | flops 2952790016 | bytes 12845056 | tf_op jit(solution)/shard_map/iecd,edf->iecf/dot_general | solution.py:54
  121.7 23.4 %all-gather.8.cloned.1.call-done = bf16[2,2048,704]{1,2,0:T(8,128)(2,1)} async-done(((bf16[2,2048,176]{1,2,0:T(8,128)(2,1)}), bf16[2,2048,704]{1,2,0:T(8,128)(2,1)}) %all-gather.8.cloned.1.call-update) | async-done | bytes 5767184 | tf_op jit(solution)/shard_map/all_gather | solution.py:52
  145.0 13.1 %convert_bitcast_fusion = bf16[8,2,64,2048]{3,2,0,1:T(8,128)(2,1)} fusion(bf16[2,2048,704]{1,2,0:T(8,128)(2,1)} %all-gather.8.cloned.1.call-done, f32[2,8,64,704]{3,2,1,0:T(8,128)} %fusion.2, bf16[2,2048,704]{1,2,0:T(8,128)(2,1)} %all-gather.4.cloned.1.call-done, bf16[8,2,64,2048]{3,2,1,0:T(8,128)(2,1)} %all_to_all.29), kind=kOutput, calls=%fused_computation.8 | convolution fusion | flops 5912002560 | bytes 22806528 | tf_op jit(solution)/shard_map/iecf,edf->iecd/dot_general | solution.py:56
  158.2 4.8 %copy.39 = bf16[8,2,64,2048]{3,2,1,0:T(8,128)(2,1)} copy(bf16[8,2,64,2048]{3,2,0,1:T(8,128)(2,1)} %convert_bitcast_fusion) | data formatting | bytes 8388608 | tf_op jit(solution)/shard_map/convert_element_type | solution.py:58
  162.9 5.5 %all-to-all-start.2 = ((bf16[8,2,64,2048]{3,2,1,0:T(8,128)(2,1)}), bf16[8,2,64,2048]{3,2,1,0:T(8,128)(2,1)}, u32[]{:S(2)}, u32[]{:S(2)}) async-start(bf16[8,2,64,2048]{3,2,1,0:T(8,128)(2,1)} %copy.39), calls=%async_computation.2 | async-start | bytes 8388608 | tf_op jit(solution)/shard_map/all_to_all | solution.py:59
  168.4 0.0 collective-permute-start
  168.4 8.6 %collective-permute-done = bf16[128,2048]{1,0:T(8,128)(2,1)S(1)} collective-permute-done((bf16[128,2048]{1,0:T(8,128)(2,1)S(1)}, bf16[128,2048]{1,0:T(8,128)(2,1)S(1)}, u32[]{:S(2)}, u32[]{:S(2)}) %collective-permute-start) | collective-permute-done | bytes 524320 | tf_op jit(solution)/shard_map/ppermute | solution.py:65
  177.0 0.0 collective-permute-start.1
  177.0 8.6 %collective-permute-done.1 = bf16[128,2048]{1,0:T(8,128)(2,1)S(1)} collective-permute-done((bf16[128,2048]{1,0:T(8,128)(2,1)S(1)}, bf16[128,2048]{1,0:T(8,128)(2,1)S(1)}, u32[]{:S(2)}, u32[]{:S(2)}) %collective-permute-start.1) | collective-permute-done | bytes 524320 | tf_op jit(solution)/shard_map/ppermute | solution.py:65
  185.6 0.0 collective-permute-start.2
  185.7 0.7 copy.40
  186.4 1.0 reshape.66
  187.4 0.7 broadcast_select_fusion
  188.1 0.7 copy.41
  188.8 1.4 copy.36
  190.2 4.0 %collective-permute-done.2 = bf16[128,2048]{1,0:T(8,128)(2,1)S(1)} collective-permute-done((bf16[128,2048]{1,0:T(8,128)(2,1)S(1)}, bf16[128,2048]{1,0:T(8,128)(2,1)S(1)}, u32[]{:S(2)}, u32[]{:S(2)}) %collective-permute-start.2) | collective-permute-done | bytes 524320 | tf_op jit(solution)/shard_map/ppermute | solution.py:65
  194.4 0.9 constant_dynamic-update-slice_fusion.4
  195.3 0.0 copy-start.10
  195.4 1.0 constant_dynamic-update-slice_fusion
  196.4 1.0 fusion.28
  197.4 1.0 fusion.34
  198.4 0.8 copy.55
  199.2 62.9 %all-to-all-done.2 = bf16[8,2,64,2048]{3,2,1,0:T(8,128)(2,1)} async-done(((bf16[8,2,64,2048]{3,2,1,0:T(8,128)(2,1)}), bf16[8,2,64,2048]{3,2,1,0:T(8,128)(2,1)}, u32[]{:S(2)}, u32[]{:S(2)}) %all-to-all-start.2) | async-done | bytes 4194336 | tf_op jit(solution)/shard_map/all_to_all | solution.py:59
  262.1 3.5 %all-to-all-start = ((bf16[4,128,352]{1,2,0:T(8,128)(2,1)}), bf16[4,128,352]{1,2,0:T(8,128)(2,1)S(1)}, u32[]{:S(2)}, u32[]{:S(2)}) async-start(bf16[4,128,352]{1,2,0:T(8,128)(2,1)} %bitcast.59), calls=%async_computation | async-start | bytes 720896 | tf_op jit(solution)/shard_map/all_to_all | solution.py:72
  265.6 9.8 %gather_fusion = bf16[768,2048]{1,0:T(8,128)(2,1)} fusion(bf16[1024,2048]{1,0:T(8,128)(2,1)} %bitcast.12, s32[1024]{0:T(1024)S(1)} %pad_clamp_fusion), kind=kCustom, calls=%fused_computation | custom fusion | bytes 6294528 | tf_op jit(solution)/shard_map/jit(_take)/gather | solution.py:75
  275.4 6.3 %gather.7 = bf16[128,6,2048]{2,1,0:T(8,128)(2,1)} reshape(bf16[768,2048]{1,0:T(8,128)(2,1)} %gather_fusion) | data formatting | bytes 6291456 | tf_op jit(solution)/shard_map/jit(_take)/gather | solution.py:75
  281.7 0.0 copy-done.2
  281.7 6.0 %multiply_reduce_fusion = f32[128,2048]{1,0:T(8,128)S(1)} fusion(f32[128,6]{1,0:T(8,128)S(1)} %copy-done.2, bf16[128,6,2048]{2,1,0:T(8,128)(2,1)} %gather.7, pred[128,6]{1,0:T(8,128)(4,1)S(1)} %copy-done.4), kind=kLoop, calls=%fused_computation.1 | loop fusion | flops 6029312 | bytes 4198144 | tf_op jit(solution)/shard_map/reduce_sum | solution.py:79
  287.7 0.0 all-to-all-done
  287.7 4.4 %fusion.17 = bf16[128,2048]{1,0:T(8,128)(2,1)} fusion(f32[128,2048]{1,0:T(8,128)S(1)} %multiply_reduce_fusion, bf16[128,1408]{0,1:T(8,128)(2,1)S(1)} %bitcast.61, bf16[1408,2048]{1,0:T(8,128)(2,1)} %param.23, bf16[128,2048]{1,0:T(8,128)(2,1)S(1)} %copy-done.1), kind=kOutput, calls=%fused_computation.24 | convolution fusion | flops 739246080 | bytes 8224768 | tf_op jit(solution)/shard_map/dot_general | solution.py:73
  (25 shorter events, 0.3 us)
Async XLA Ops:
  6.5 189.8 %copy-start = (bf16[2048,352]{0,1:T(8,128)(2,1)S(1)}, bf16[2048,352]{0,1:T(8,128)(2,1)}, u32[]{:S(2)}) copy-start(bf16[2048,352]{0,1:T(8,128)(2,1)} %param.21) | copy-start | bytes 4325380
  6.5 2.2 copy-start.1
  6.5 3.0 %copy-start.3 = (f32[2048]{0:T(1024)S(1)}, f32[2048]{0:T(1024)}, u32[]{:S(2)}) copy-start(f32[2048]{0:T(1024)} %param.13) | copy-start | bytes 24580
  6.5 3.2 %copy-start.8 = (s32[128,6]{0,1:T(8,128)S(1)}, s32[128,6]{0,1:T(8,128)}, u32[]{:S(2)}) copy-start(s32[128,6]{0,1:T(8,128)} %param.14) | copy-start | bytes 9220
  6.5 3.2 %copy-start.7 = (s32[128,6]{0,1:T(8,128)S(1)}, s32[128,6]{0,1:T(8,128)}, u32[]{:S(2)}) copy-start(s32[128,6]{0,1:T(8,128)} %param.15) | copy-start | bytes 9220
  6.5 3.2 %copy-start.9 = (s32[128,6]{0,1:T(8,128)S(1)}, s32[128,6]{0,1:T(8,128)}, u32[]{:S(2)}) copy-start(s32[128,6]{0,1:T(8,128)} %param.16) | copy-start | bytes 9220
  6.6 106.1 %all-gather.6.cloned.1.call-start = ((), (), s32[]{:S(2)}) async-start(), calls=%async_computation.4 | async-start | bytes 7208960 | tf_op jit(solution)/shard_map/all_gather | solution.py:51
  7.3 114.4 %all-gather.4.cloned.1.call-start = ((), (), s32[]{:S(2)}) async-start(), calls=%async_computation.3 | async-start | bytes 7208960 | tf_op jit(solution)/shard_map/all_gather | solution.py:50
  8.0 137.0 %all-gather.8.cloned.1.call-start = ((), (), s32[]{:S(2)}) async-start(), calls=%async_computation.5 | async-start | bytes 7208960 | tf_op jit(solution)/shard_map/all_gather | solution.py:52
  9.0 0.6 copy-start.6
  10.4 102.3 %copy-start.5 = (pred[128,6]{0,1:T(8,128)(4,1)}, pred[128,6]{0,1:T(8,128)(4,1)S(1)}, u32[]{:S(2)}) copy-start(pred[128,6]{0,1:T(8,128)(4,1)S(1)} %get-tuple-element.8) | copy-start | bytes 2308
  162.9 99.2 %all-to-all-start.2 = ((bf16[8,2,64,2048]{3,2,1,0:T(8,128)(2,1)}), bf16[8,2,64,2048]{3,2,1,0:T(8,128)(2,1)}, u32[]{:S(2)}, u32[]{:S(2)}) async-start(bf16[8,2,64,2048]{3,2,1,0:T(8,128)(2,1)} %copy.39), calls=%async_computation.2 | async-start | bytes 8388608 | tf_op jit(solution)/shard_map/all_to_all | solution.py:59
  168.4 8.6 %collective-permute-start = (bf16[128,2048]{1,0:T(8,128)(2,1)S(1)}, bf16[128,2048]{1,0:T(8,128)(2,1)S(1)}, u32[]{:S(2)}, u32[]{:S(2)}) collective-permute-start(bf16[128,2048]{1,0:T(8,128)(2,1)S(1)} %fusion.33), channel_id=1, source_target_pairs={{0,1},{1,2},{2,3},{3,0},{4,5},{5,6},{6,7},{7,4},{8,9},{9,10},{10,1... | collective-permute-start | bytes 1572872 | tf_op jit(solution)/shard_map/ppermute | solution.py:65
  177.0 8.6 %collective-permute-start.1 = (bf16[128,2048]{1,0:T(8,128)(2,1)S(1)}, bf16[128,2048]{1,0:T(8,128)(2,1)S(1)}, u32[]{:S(2)}, u32[]{:S(2)}) collective-permute-start(bf16[128,2048]{1,0:T(8,128)(2,1)S(1)} %collective-permute-done), channel_id=1, source_target_pairs={{0,1},{1,2},{2,3},{3,0},{4,5},{5,6},{6,7},{7,4},{8,9},{9,10},{10,1... | collective-permute-start | bytes 1572872 | tf_op jit(solution)/shard_map/ppermute | solution.py:65
  185.6 8.6 %collective-permute-start.2 = (bf16[128,2048]{1,0:T(8,128)(2,1)S(1)}, bf16[128,2048]{1,0:T(8,128)(2,1)S(1)}, u32[]{:S(2)}, u32[]{:S(2)}) collective-permute-start(bf16[128,2048]{1,0:T(8,128)(2,1)S(1)} %collective-permute-done.1), channel_id=1, source_target_pairs={{0,1},{1,2},{2,3},{3,0},{4,5},{5,6},{6,7},{7,4},{8,9},{9,10},{10,1... | collective-permute-start | bytes 1572872 | tf_op jit(solution)/shard_map/ppermute | solution.py:65
  195.3 2.1 copy-start.10
  262.1 25.6 %all-to-all-start = ((bf16[4,128,352]{1,2,0:T(8,128)(2,1)}), bf16[4,128,352]{1,2,0:T(8,128)(2,1)S(1)}, u32[]{:S(2)}, u32[]{:S(2)}) async-start(bf16[4,128,352]{1,2,0:T(8,128)(2,1)} %bitcast.59), calls=%async_computation | async-start | bytes 720896 | tf_op jit(solution)/shard_map/all_to_all | solution.py:72
  275.4 6.3 %copy-start.2 = (f32[128,6]{1,0:T(8,128)S(1)}, f32[128,6]{1,0:T(8,128)}, u32[]{:S(2)}) copy-start(f32[128,6]{1,0:T(8,128)} %copy.41) | copy-start | bytes 9220
  275.4 6.3 %copy-start.4 = (pred[128,6]{1,0:T(8,128)(4,1)S(1)}, pred[128,6]{1,0:T(8,128)(4,1)}, u32[]{:S(2)}) copy-start(pred[128,6]{1,0:T(8,128)(4,1)} %copy.36) | copy-start | bytes 2308
Sparse Core Ops, SparseCore 0:
  8.9 46.0 all-gather.5
  56.6 43.3 all-gather.3
  101.6 43.3 all-gather.7
